TPU v7x, 32 devices: a whole 2x2x4 slice. The times are simulated.
32 devices in a mesh: row: 8 (over z, x), col: 4 (over y, core).
Axes of the slice: x: 2, y: 2, z: 4, core: 2. Of those that a mesh axis runs over, the one named last changes fastest.
Arguments:
- panel_block: float32 [20480, 512], P('row', 'col'), may hold values from -12 to 12
- trailing: float32 [20480, 20480], P('row', 'col'), may hold values from -6 to 6
Outputs:
- updated: float32 [20480, 20480], P('row', 'col')
All inputs are finite; a program needn't handle non-finite values.
Results may differ from a plain program's by a relative error of at most 0.0003.
Values sent between devices are 32-bit elements; how exact they have to be, the bound alone decides.
No kernel may reach another device: no remote copies, remote signals or barrier semaphores. Data moves between devices by JAX's collectives and lax.ppermute only.
A program may use at most 192 MiB of HBM per device.

v0:
```python
import jax
import jax.numpy as jnp
from jax import lax
from jax.sharding import PartitionSpec as P

N = 20480


def on_device(panel_block, trailing):
    local_rows = panel_block.shape[0]
    local_width = panel_block.shape[1]
    rows_count = lax.axis_size("row")
    cols_count = lax.axis_size("col")
    copies = rows_count // cols_count
    row_owner = lax.axis_index("row")
    col_owner = lax.axis_index("col")
    mc_rows = lax.all_gather(panel_block, "col", axis=1, tiled=True)
    squares = lax.psum(jnp.sum(mc_rows * mc_rows), "row")
    column_block = lax.all_gather(panel_block, "row", axis=0, tiled=True)
    shaped = column_block.reshape(copies, cols_count, local_rows, local_width)
    moved = lax.all_to_all(shaped, "col", split_axis=1, concat_axis=3, tiled=True)
    stacked = moved.reshape(copies, local_rows, mc_rows.shape[1])
    mr_rows = jnp.transpose(stacked, (1, 0, 2)).reshape(copies * local_rows, stacked.shape[2])
    update = lax.dot_general(
        mc_rows,
        mr_rows,
        (((1,), (1,)), ((), ())),
        precision=lax.Precision.HIGHEST,
        preferred_element_type=jnp.float32,
    )
    row_index = jnp.arange(local_rows, dtype=jnp.int32) * rows_count + row_owner
    col_index = jnp.arange(mr_rows.shape[0], dtype=jnp.int32) * cols_count + col_owner
    lower_part = row_index[:, None] >= col_index[None, :]
    factor = 0.8 * jnp.sqrt(jnp.float32(N)) / jnp.sqrt(squares + 1e-06)
    return trailing - factor * jnp.where(lower_part, update, jnp.zeros_like(update))


def solution(mesh):
    in_specs = (P("row", "col"), P("row", "col"))
    out_specs = P("row", "col")
    return jax.shard_map(
        on_device, mesh=mesh, in_specs=in_specs, out_specs=out_specs, check_vma=False
    )
```

profile of v0, /device:TPU:0, one launch (start us, length us, event | category | flops | bytes accessed | tf_op | source)
XLA Modules:
  0.0 456.7 jit_solution(3020572873124051038)
XLA Ops:
  6.5 0.0 all-gather.5.cloned.1.call-start
  6.5 0.7 all-gather.5.cloned.1.call-update
  7.3 0.0 all-gather.3.cloned.1.call-start
  7.3 0.7 all-gather.3.cloned.1.call-update
  8.0 154.8 %all-gather.5.cloned.1.call-done = f32[20480,128]{1,0:T(8,128)} async-done(((f32[2560,128]{1,0:T(8,128)}), f32[20480,128]{1,0:T(8,128)}) %all-gather.5.cloned.1.call-update) | async-done | bytes 10485776 | tf_op jit(solution)/shard_map/all_gather | solution.py:19
  162.8 9.6 %copy.6 = f32[2,4,2560,128]{3,2,0,1:T(8,128)} copy(f32[2,4,2560,128]{3,2,1,0:T(8,128)} %bitcast.11) | data formatting | bytes 20971520 | tf_op jit(solution)/shard_map/reshape | solution.py:20
  172.4 6.0 %all-to-all-start = ((f32[2,4,2560,128]{3,2,0,1:T(8,128)}), f32[2,4,2560,128]{3,2,0,1:T(8,128)}, u32[]{:S(2)}, u32[]{:S(2)}) async-start(f32[2,4,2560,128]{3,2,0,1:T(8,128)} %copy.6), calls=%async_computation | async-start | bytes 20971520 | tf_op jit(solution)/shard_map/all_to_all | solution.py:21
  178.5 45.0 %all-gather.3.cloned.1.call-done = f32[2560,512]{1,0:T(8,128)} async-done(((f32[2560,128]{1,0:T(8,128)}), f32[2560,512]{1,0:T(8,128)}) %all-gather.3.cloned.1.call-update) | async-done | bytes 5242896 | tf_op jit(solution)/shard_map/all_gather | solution.py:17
  223.4 4.5 multiply_reduce_fusion
  227.9 25.2 %psum.7 = f32[]{:T(128)} all-reduce(f32[]{:T(128)} %multiply_reduce_fusion), channel_id=1, replica_groups=mesh['row'=8,'col'=4] {'row'}, use_global_device_ids=true, to_apply=%region_1.0 | all-reduce | flops 1 | bytes 8 | tf_op jit(solution)/shard_map/psum | solution.py:18
  253.8 60.0 %all-to-all-done = f32[2,4,2560,128]{3,2,0,1:T(8,128)} async-done(((f32[2,4,2560,128]{3,2,0,1:T(8,128)}), f32[2,4,2560,128]{3,2,0,1:T(8,128)}, u32[]{:S(2)}, u32[]{:S(2)}) %all-to-all-start) | async-done | bytes 10485792 | tf_op jit(solution)/shard_map/all_to_all | solution.py:21
  313.8 11.4 %copy.7 = f32[2,4,2560,128]{2,3,1,0:T(8,128)} copy(f32[2,4,2560,128]{3,2,0,1:T(8,128)} %all-to-all-done) | data formatting | bytes 20971520 | tf_op jit(solution)/shard_map/all_to_all | solution.py:21
  325.2 16.1 %copy.8 = f32[2560,2,512]{2,1,0:T(2,128)} copy(f32[2560,2,512]{0,2,1:T(8,128)} %bitcast.10) | data formatting | bytes 20971520 | tf_op jit(solution)/shard_map/transpose | solution.py:23
  341.3 13.3 %reshape.22 = f32[5120,512]{1,0:T(8,128)} reshape(f32[2560,2,512]{2,1,0:T(2,128)} %copy.8) | data formatting | bytes 20971520 | tf_op jit(solution)/shard_map/reshape | solution.py:23
  354.5 95.4 %multiply_subtract_fusion = f32[2560,5120]{1,0:T(8,128)} fusion(f32[2560,5120]{1,0:T(8,128)} %param.3, f32[2560,512]{1,0:T(8,128)} %all-gather.3.cloned.1.call-done, f32[5120,512]{1,0:T(8,128)} %reshape.22, s32[5120]{0:T(1024)S(1)} %multiply_add_fusion, f32[]{:T(128)S(6)} %div.3, s32[2560]{0:T(1024)S(1)} %multiply_add_fusion.1), kind=kOutput, calls=%fused_computation | convolution fusion | flops 80583065600 | bytes 120616960 | tf_op jit(solution)/shard_map/dot_general | solution.py:24
  (2 shorter events, 0.0 us)
Async XLA Ops:
  6.5 156.2 %all-gather.5.cloned.1.call-start = ((), (), s32[]{:S(2)}) async-start(), calls=%async_computation.2 | async-start | bytes 11796480 | tf_op jit(solution)/shard_map/all_gather | solution.py:19
  7.3 216.2 %all-gather.3.cloned.1.call-start = ((), (), s32[]{:S(2)}) async-start(), calls=%async_computation.1 | async-start | bytes 6553600 | tf_op jit(solution)/shard_map/all_gather | solution.py:17
  172.4 141.4 %all-to-all-start = ((f32[2,4,2560,128]{3,2,0,1:T(8,128)}), f32[2,4,2560,128]{3,2,0,1:T(8,128)}, u32[]{:S(2)}, u32[]{:S(2)}) async-start(f32[2,4,2560,128]{3,2,0,1:T(8,128)} %copy.6), calls=%async_computation | async-start | bytes 20971520 | tf_op jit(solution)/shard_map/all_to_all | solution.py:21
Sparse Core Ops, SparseCore 0:
  9.5 153.2 all-gather.4
  164.3 59.0 all-gather.2
where the time goes:
time: 458 us; the launch traced here: 457 us
  waiting for transfers between devices  261 us (57%)
  matrix products  95.4 us (21%)
  local copies, waits for them, and re-layouts  50.4 us (11%)
  blocking collectives  25.2 us (6%)
  between operations  14.1 us (3%)
  starting transfers between devices  6.08 us (1%)
    all_gather x1, waiting for transfers between devices, on_device(): column_block = lax.all_gather(panel_block, 'row', axis=0, tiled=True)  155 us
    dot_general x1, matrix products, on_device(): lax.dot_general(mc_rows, mr_rows, (((1,), (1,)), ((), ())), precision=lax...  95.4 us
    all_to_all x1, waiting for transfers between devices, on_device(): lax.all_to_all(shaped, 'col', split_axis=1, concat_axis=3, tiled=True)  60 us
    all_gather x1, waiting for transfers between devices, on_device(): mc_rows = lax.all_gather(panel_block, 'col', axis=1, tiled=True)  45 us
    psum x1, blocking collectives, on_device(): squares = lax.psum(jnp.sum(mc_rows * mc_rows), 'row')  25.2 us
    transpose x1, local copies, waits for them, and re-layouts, on_device(): jnp.transpose(stacked, (1, 0, 2))  16.1 us
    reshape x1, local copies, waits for them, and re-layouts, on_device(): jnp.transpose(stacked, (1, 0, 2))  13.3 us
    all_to_all x1, local copies, waits for them, and re-layouts, on_device(): lax.all_to_all(shaped, 'col', split_axis=1, concat_axis=3, tiled=True)  11.4 us
  transfers between devices with their start and end apart: 3, of which 3 were waited for; matrix products, arithmetic and copies ran while one was open for 3% of the time, Pallas kernels for 0%

commit v1 on v0

--- a/solution.py
+++ b/solution.py
@@ -18,7 +18,9 @@
     squares = lax.psum(jnp.sum(mc_rows * mc_rows), "row")
     column_block = lax.all_gather(panel_block, "row", axis=0, tiled=True)
     shaped = column_block.reshape(copies, cols_count, local_rows, local_width)
-    moved = lax.all_to_all(shaped, "col", split_axis=1, concat_axis=3, tiled=True)
+    moved = jnp.concatenate(
+        lax.all_to_all(jnp.stack(jnp.split(shaped, lax.axis_size("col"), 1)), "col", 0, 0), 3
+    )
     stacked = moved.reshape(copies, local_rows, mc_rows.shape[1])
     mr_rows = jnp.transpose(stacked, (1, 0, 2)).reshape(copies * local_rows, stacked.shape[2])
     update = lax.dot_general(

time: 458 us -> 511 us (1.12)
  local copies, waits for them, and re-layouts: 50.4 us -> 150 us
  waiting for transfers between devices: 261 us -> 209 us
    sub x0 -> x1, local copies, waits for them, and re-layouts: none -> 52 us  [on_device(): trailing - factor * jnp.where(lower_part, update, jnp.zeros_like(update))]
    unnamed x0 -> x1, local copies, waits for them, and re-layouts: none -> 52 us
    all_to_all x1, waiting for transfers between devices: 60 us -> 8.12 us  [on_device(): lax.all_to_all(jnp.stack(jnp.split(shaped, lax.axis_size('col'), 1)), 'co...]
    all_to_all x1 -> x0, local copies, waits for them, and re-layouts: 11.4 us -> none  [on_device(): lax.all_to_all(shaped, 'col', split_axis=1, concat_axis=3, tiled=True)]
  transfers between devices with their start and end apart: 3 -> 3, of which waited for: 3 -> 3; matrix products, arithmetic and copies ran while one was open for 3% -> 13% of each run, Pallas kernels for 0% -> 0%
where the time goes in v1:
time: 511 us; the launch traced here: 509 us
  waiting for transfers between devices  209 us (41%)
  local copies, waits for them, and re-layouts  150 us (29%)
  matrix products  95.3 us (19%)
  blocking collectives  25.1 us (5%)
  between operations  14.2 us (3%)
  other arithmetic  9.47 us (2%)
  starting transfers between devices  6.08 us (1%)
    all_gather x1, waiting for transfers between devices, on_device(): column_block = lax.all_gather(panel_block, 'row', axis=0, tiled=True)  155 us
    dot_general x1, matrix products, on_device(): lax.dot_general(mc_rows, mr_rows, (((1,), (1,)), ((), ())), precision=lax...  95.3 us
    sub x1, local copies, waits for them, and re-layouts, on_device(): trailing - factor * jnp.where(lower_part, update, jnp.zeros_like(update))  52 us
    unnamed x1, local copies, waits for them, and re-layouts  52 us
    all_gather x1, waiting for transfers between devices, on_device(): mc_rows = lax.all_gather(panel_block, 'col', axis=1, tiled=True)  44.6 us
    psum x1, blocking collectives, on_device(): squares = lax.psum(jnp.sum(mc_rows * mc_rows), 'row')  25.1 us
    transpose x1, local copies, waits for them, and re-layouts, on_device(): jnp.transpose(stacked, (1, 0, 2))  16.1 us
    reshape x1, local copies, waits for them, and re-layouts, on_device(): jnp.transpose(stacked, (1, 0, 2))  13.3 us
  transfers between devices with their start and end apart: 3, of which 3 were waited for; matrix products, arithmetic and copies ran while one was open for 13% of the time, Pallas kernels for 0%

profile of v1, /device:TPU:0, one launch (start us, length us, event | category | flops | bytes accessed | tf_op | source)
XLA Modules:
  0.0 508.8 jit_solution(515382029829197417)
XLA Ops:
  6.5 0.0 all-gather.5.cloned.1.call-start
  6.5 0.7 all-gather.5.cloned.1.call-update
  7.3 0.0 all-gather.3.cloned.1.call-start
  7.3 0.7 all-gather.3.cloned.1.call-update
  8.0 154.8 %all-gather.5.cloned.1.call-done = f32[20480,128]{1,0:T(8,128)} async-done(((f32[2560,128]{1,0:T(8,128)}), f32[20480,128]{1,0:T(8,128)}) %all-gather.5.cloned.1.call-update) | async-done | bytes 10485776 | tf_op jit(solution)/shard_map/all_gather | solution.py:19
  162.8 4.8 slice_bitcast_fusion.3
  167.6 4.9 pad_maximum_fusion
  172.6 6.0 %all-to-all-start = ((f32[4,2,1,2560,128]{4,3,1,2,0:T(8,128)}), f32[4,2,1,2560,128]{4,3,1,2,0:T(8,128)}, u32[]{:S(2)}, u32[]{:S(2)}) async-start(f32[4,2,1,2560,128]{4,3,1,2,0:T(8,128)} %pad_maximum_fusion), calls=%async_computation | async-start | bytes 20971520 | tf_op jit(solution)/shard_map/all_to_all | solution.py:22
  178.6 44.6 %all-gather.3.cloned.1.call-done = f32[2560,512]{1,0:T(8,128)} async-done(((f32[2560,128]{1,0:T(8,128)}), f32[2560,512]{1,0:T(8,128)}) %all-gather.3.cloned.1.call-update) | async-done | bytes 5242896 | tf_op jit(solution)/shard_map/all_gather | solution.py:17
  223.2 4.5 multiply_reduce_fusion
  227.8 52.0 %copy.19 = f32[2560,5120]{0,1:T(8,128)} copy(f32[2560,5120]{1,0:T(8,128)} %param.3) | data formatting | bytes 104857600 | tf_op args[1]
  279.8 25.1 %psum.7 = f32[]{:T(128)} all-reduce(f32[]{:T(128)} %multiply_reduce_fusion), channel_id=1, replica_groups=mesh['row'=8,'col'=4] {'row'}, use_global_device_ids=true, to_apply=%region_1.0 | all-reduce | flops 1 | bytes 8 | tf_op jit(solution)/shard_map/psum | solution.py:18
  305.6 8.1 %all-to-all-done = f32[4,2,1,2560,128]{4,3,1,2,0:T(8,128)} async-done(((f32[4,2,1,2560,128]{4,3,1,2,0:T(8,128)}), f32[4,2,1,2560,128]{4,3,1,2,0:T(8,128)}, u32[]{:S(2)}, u32[]{:S(2)}) %all-to-all-start) | async-done | bytes 10485792 | tf_op jit(solution)/shard_map/all_to_all | solution.py:22
  313.8 11.5 %copy.17 = f32[2,1,2560,4,128]{2,4,3,0,1:T(8,128)} copy(f32[2,1,2560,4,128]{4,2,0,1,3:T(8,128)} %bitcast.5) | data formatting | bytes 20971520 | tf_op jit(solution)/shard_map/reshape | solution.py:21
  325.3 16.1 %copy.18 = f32[2560,2,512]{2,1,0:T(2,128)} copy(f32[2560,2,512]{0,2,1:T(8,128)} %bitcast.27) | data formatting | bytes 20971520 | tf_op jit(solution)/shard_map/transpose | solution.py:25
  341.4 13.3 %reshape.21 = f32[5120,512]{1,0:T(8,128)} reshape(f32[2560,2,512]{2,1,0:T(2,128)} %copy.18) | data formatting | bytes 20971520 | tf_op jit(solution)/shard_map/reshape | solution.py:25
  354.6 95.3 %fusion.1 = f32[2560,5120]{0,1:T(8,128)} fusion(f32[2560,5120]{0,1:T(8,128)} %copy.19, f32[5120,512]{1,0:T(8,128)} %reshape.21, f32[2560,512]{1,0:T(8,128)} %all-gather.3.cloned.1.call-done, s32[2560]{0:T(1024)S(1)} %multiply_add_fusion.1, f32[]{:T(128)S(6)} %div.3, s32[5120]{0:T(1024)S(1)} %multiply_add_fusion), kind=kOutput, calls=%fused_computation.2 | convolution fusion | flops 80583065600 | bytes 120616960 | tf_op jit(solution)/shard_map/dot_general | solution.py:26
  449.9 52.0 %copy.20 = f32[2560,5120]{1,0:T(8,128)} copy(f32[2560,5120]{0,1:T(8,128)} %fusion.1) | data formatting | bytes 104857600 | tf_op jit(solution)/shard_map/sub | solution.py:37
  (2 shorter events, 0.0 us)
Async XLA Ops:
  6.5 156.2 %all-gather.5.cloned.1.call-start = ((), (), s32[]{:S(2)}) async-start(), calls=%async_computation.2 | async-start | bytes 11796480 | tf_op jit(solution)/shard_map/all_gather | solution.py:19
  7.3 216.0 %all-gather.3.cloned.1.call-start = ((), (), s32[]{:S(2)}) async-start(), calls=%async_computation.1 | async-start | bytes 6553600 | tf_op jit(solution)/shard_map/all_gather | solution.py:17
  172.6 141.2 %all-to-all-start = ((f32[4,2,1,2560,128]{4,3,1,2,0:T(8,128)}), f32[4,2,1,2560,128]{4,3,1,2,0:T(8,128)}, u32[]{:S(2)}, u32[]{:S(2)}) async-start(f32[4,2,1,2560,128]{4,3,1,2,0:T(8,128)} %pad_maximum_fusion), calls=%async_computation | async-start | bytes 20971520 | tf_op jit(solution)/shard_map/all_to_all | solution.py:22
Sparse Core Ops, SparseCore 0:
  9.5 153.2 all-gather.4
  164.3 58.8 all-gather.2
